TPU v7x, 32 devices: a whole 2x2x4 slice. The times are simulated.
32 devices in a mesh: fsdp: 4 (over y, x), tp: 8 (over z, core).
Axes of the slice: x: 2, y: 2, z: 4, core: 2. Of those that a mesh axis runs over, the one named last changes fastest.
Arguments:
- tokens: bfloat16 [1024, 8192], P('fsdp', 'tp'), may hold values from -6 to 6
- out_grad: bfloat16 [1024, 8192], P('fsdp', 'tp'), may hold values from -6 to 6
- gate_weight: bfloat16 [8192, 1024], P('fsdp', 'tp'), may hold values from -0.0625 to 0.0625
- up_weight: bfloat16 [8192, 1024], P('fsdp', 'tp'), may hold values from -0.0625 to 0.0625
- down_weight: bfloat16 [1024, 8192], P('tp', 'fsdp'), may hold values from -0.1875 to 0.1875
Outputs:
- input_grad: bfloat16 [1024, 8192], P('fsdp', 'tp')
- gate_grad: float32 [8192, 1024], P('fsdp', 'tp')
- up_grad: float32 [8192, 1024], P('fsdp', 'tp')
- down_grad: float32 [1024, 8192], P('tp', 'fsdp')
All inputs are finite; a program needn't handle non-finite values.
Results may differ from a plain program's by a relative error of at most 0.0023.
Values may be sent and summed in bfloat16 or wider, within the bound.
A program may use at most 128 MiB of HBM per device.

v0:
```python
import math
import jax
import jax.numpy as jnp
from jax import lax
from jax.sharding import PartitionSpec as P


def over_all(shard, axis, dim, absorb, state):
    everything = jax.tree.map(lambda a: lax.all_gather(a, axis, axis=dim, tiled=True), shard)
    return absorb(state, everything, jnp.int32(0))


def own_rows(portion, rows, axis):
    count = rows * lax.axis_size(axis)
    return lax.psum_scatter(portion(jnp.int32(0), count), axis, scatter_dimension=0, tiled=True)


def column_term(left, right, start, count, factor):
    block = lax.dynamic_slice_in_dim(left, start, count, 1)
    product = lax.dot_general(
        block, right, (((0,), (0,)), ((), ())), preferred_element_type=jnp.float32
    )
    return product * factor


def body(tokens, out_grad, gate_weight, up_weight, down_weight):
    factor = 1.0 / math.sqrt(tokens.shape[0] * lax.axis_size("fsdp"))
    whole = lax.all_gather(tokens, "tp", axis=1, tiled=True)
    grads = lax.all_gather(out_grad, "tp", axis=1, tiled=True)
    gate_full, up_full = (
        lax.all_gather(gate_weight, "fsdp", axis=0, tiled=True),
        lax.all_gather(up_weight, "fsdp", axis=0, tiled=True),
    )
    gate = jnp.dot(whole, gate_full, preferred_element_type=jnp.float32)
    up = jnp.dot(whole, up_full, preferred_element_type=jnp.float32)

    def add_down(total, piece, start):
        columns = lax.dynamic_slice_in_dim(grads, start, piece.shape[1], 1)
        return total + lax.dot_general(
            columns, piece, (((1,), (1,)), ((), ())), preferred_element_type=jnp.float32
        )

    initial = jnp.zeros((whole.shape[0], down_weight.shape[0]), jnp.float32)
    hidden_grad = over_all(down_weight, "fsdp", 1, add_down, initial)
    squashed = jax.nn.sigmoid(gate)
    activated = gate * squashed
    slope = squashed * (1.0 + gate * (1.0 - squashed))
    hidden = (activated * up).astype(jnp.bfloat16)
    gate_delta = (hidden_grad * up * slope).astype(jnp.bfloat16)
    up_delta = (hidden_grad * activated).astype(jnp.bfloat16)
    partial_term = jnp.dot(gate_delta, gate_full.T, preferred_element_type=jnp.float32)
    partial_term = partial_term + jnp.dot(up_delta, up_full.T, preferred_element_type=jnp.float32)
    input_grad = lax.psum_scatter(partial_term, "tp", scatter_dimension=1, tiled=True).astype(
        jnp.bfloat16
    )
    rows_here = gate_weight.shape[0]

    def joint_term(start, count):
        return jnp.concatenate(
            [
                column_term(whole, gate_delta, start, count, factor),
                column_term(whole, up_delta, start, count, factor),
                column_term(grads, hidden, start, count, factor),
            ],
            axis=1,
        )

    summed = own_rows(joint_term, rows_here, "fsdp")
    width = gate_delta.shape[1]
    gate_grad = summed[:, :width]
    up_grad = summed[:, width : 2 * width]
    down_grad = summed[:, 2 * width :].T
    return (input_grad, gate_grad, up_grad, down_grad)


def solution(mesh):
    return jax.shard_map(
        body,
        mesh=mesh,
        in_specs=(
            P("fsdp", "tp"),
            P("fsdp", "tp"),
            P("fsdp", "tp"),
            P("fsdp", "tp"),
            P("tp", "fsdp"),
        ),
        out_specs=(P("fsdp", "tp"), P("fsdp", "tp"), P("fsdp", "tp"), P("tp", "fsdp")),
        check_vma=False,
    )
```

profile of v0, /device:TPU:0, one launch (start us, length us, event | category | flops | bytes accessed | tf_op | source)
XLA Modules:
  0.0 450.8 jit_solution(9459281939705098741)
XLA Ops:
  7.2 0.7 all-gather.14.cloned.1.call-update
  7.9 0.0 all-gather.10.cloned.1.call-start
  7.9 0.7 all-gather.10.cloned.1.call-update
  8.7 0.7 all-gather.12.cloned.1.call-update
  9.4 0.0 all-gather.8.cloned.1.call-start
  9.4 0.5 all-gather.8.cloned.1.call-update
  10.0 0.5 all-gather.6.cloned.1.call-update
  10.5 0.0 reduce-scatter.3.cloned.1.call-start
  10.6 37.2 %all-gather.14.cloned.1.call-done = bf16[8192,128]{1,0:T(8,128)(2,1)} async-done(((bf16[2048,128]{1,0:T(8,128)(2,1)}), bf16[8192,128]{1,0:T(8,128)(2,1)}) %all-gather.14.cloned.1.call-update) | async-done | bytes 2097168 | tf_op jit(solution)/shard_map/all_gather | solution.py:31
  47.8 48.5 %all-gather.10.cloned.1.call-done = bf16[256,8192]{1,0:T(8,128)(2,1)} async-done(((bf16[256,1024]{1,0:T(8,128)(2,1)}), bf16[256,8192]{1,0:T(8,128)(2,1)}) %all-gather.10.cloned.1.call-update) | async-done | bytes 4194320 | tf_op jit(solution)/shard_map/all_gather | solution.py:28
  96.3 4.1 fusion.7
  100.4 31.8 %all-gather.12.cloned.1.call-done = bf16[8192,128]{1,0:T(8,128)(2,1)} async-done(((bf16[2048,128]{1,0:T(8,128)(2,1)}), bf16[8192,128]{1,0:T(8,128)(2,1)}) %all-gather.12.cloned.1.call-update) | async-done | bytes 2097168 | tf_op jit(solution)/shard_map/all_gather | solution.py:32
  132.1 4.1 fusion.6
  136.2 32.8 %all-gather.8.cloned.1.call-done = bf16[128,8192]{1,0:T(8,128)(2,1)} async-done(((bf16[128,2048]{1,0:T(8,128)(2,1)}), bf16[128,8192]{1,0:T(8,128)(2,1)}) %all-gather.8.cloned.1.call-update) | async-done | bytes 2097168 | tf_op jit(solution)/shard_map/all_gather | solution.py:9
  169.0 48.4 %all-gather.6.cloned.1.call-done = bf16[256,8192]{1,0:T(8,128)(2,1)} async-done(((bf16[256,1024]{1,0:T(8,128)(2,1)}), bf16[256,8192]{1,0:T(8,128)(2,1)}) %all-gather.6.cloned.1.call-update) | async-done | bytes 4194320 | tf_op jit(solution)/shard_map/all_gather | solution.py:29
  217.4 4.1 multiply_convert_fusion.1
  221.5 1.3 fusion.8
  222.8 0.3 copy-done.2
  223.1 4.5 convolution_add_fusion
  227.6 0.0 reduce-scatter.5.cloned.1.call-start
  227.6 3.1 fusion.1
  230.8 0.3 copy-done
  231.1 0.8 fusion.2
  231.9 2.1 copy-done.3
  234.0 0.8 fusion
  234.8 5.0 %pad_maximum_fusion = f32[8192,384]{0,1:T(8,128)} fusion(f32[8192,128]{0,1:T(8,128)S(1)} %fusion, f32[8192,128]{0,1:T(8,128)S(1)} %fusion.1, f32[8192,128]{0,1:T(8,128)S(1)} %fusion.2), kind=kLoop, calls=%fused_computation | loop fusion | flops 6291456 | bytes 25165824 | tf_op jit(solution)/shard_map/concatenate | solution.py:59
  239.9 76.2 %reduce-scatter.3.cloned.1.call-done = f32[256,1024]{1,0:T(8,128)} async-done(((f32[256,8192]{1,0:T(8,128)}), f32[256,1024]{1,0:T(8,128)}) %reduce-scatter.3.cloned.1.call-update) | async-done | bytes 1048592 | tf_op jit(solution)/shard_map/reduce_scatter | solution.py:53
  316.1 2.1 convert_element_type.14
  318.2 120.1 %reduce-scatter.5.cloned.1.call-done = f32[2048,384]{0,1:T(8,128)} async-done(((f32[8192,384]{0,1:T(8,128)}), f32[2048,384]{0,1:T(8,128)}) %reduce-scatter.5.cloned.1.call-update) | async-done | bytes 3145744 | tf_op jit(solution)/shard_map/reduce_scatter | solution.py:15
  438.3 3.1 slice_bitcast_fusion
  441.4 1.3 copy.9
  442.7 1.3 copy.10
  (10 shorter events, 0.2 us)
Async XLA Ops:
  7.2 40.6 %all-gather.14.cloned.1.call-start = ((), (), s32[]{:S(2)}) async-start(), calls=%async_computation.6 | async-start | bytes 2621440 | tf_op jit(solution)/shard_map/all_gather | solution.py:31
  7.9 88.4 %all-gather.10.cloned.1.call-start = ((), (), s32[]{:S(2)}) async-start(), calls=%async_computation.4 | async-start | bytes 4718592 | tf_op jit(solution)/shard_map/all_gather | solution.py:28
  8.6 123.5 %all-gather.12.cloned.1.call-start = ((), (), s32[]{:S(2)}) async-start(), calls=%async_computation.5 | async-start | bytes 2621440 | tf_op jit(solution)/shard_map/all_gather | solution.py:32
  9.4 159.6 %all-gather.8.cloned.1.call-start = ((), (), s32[]{:S(2)}) async-start(), calls=%async_computation.3 | async-start | bytes 2621440 | tf_op jit(solution)/shard_map/all_gather | solution.py:9
  10.0 207.4 %all-gather.6.cloned.1.call-start = ((), (), s32[]{:S(2)}) async-start(), calls=%async_computation.2 | async-start | bytes 4718592 | tf_op jit(solution)/shard_map/all_gather | solution.py:29
  10.5 305.5 %reduce-scatter.3.cloned.1.call-start = ((), (), s32[]{:S(2)}) async-start(), calls=%async_computation.7 | async-start | bytes 9437184 | tf_op jit(solution)/shard_map/reduce_scatter | solution.py:53
  136.2 85.3 %copy-start.1 = (bf16[8192,128]{1,0:T(8,128)(2,1)S(1)}, bf16[8192,128]{1,0:T(8,128)(2,1)}, u32[]{:S(2)}) copy-start(bf16[8192,128]{1,0:T(8,128)(2,1)} %all-gather.14.cloned.1.call-done) | copy-start | bytes 6291460
  221.5 1.6 copy-start.2
  227.6 210.7 %reduce-scatter.5.cloned.1.call-start = ((), (), s32[]{:S(2)}) async-start(), calls=%async_computation.8 | async-start | bytes 15728640 | tf_op jit(solution)/shard_map/reduce_scatter | solution.py:15
  227.6 3.5 copy-start
  231.1 2.9 copy-start.3
Sparse Core Ops, SparseCore 0:
  9.8 37.8 all-gather.13
  49.4 46.8 all-gather.9
  98.1 33.9 all-gather.11
  133.8 35.1 all-gather.7
  170.5 46.8 all-gather.5
  227.7 88.3 reduce-scatter.2
  319.2 119.0 reduce-scatter.4
where the time goes:
time: 451 us
  waiting for transfers between devices  398 us (88%)
  matrix products  22.8 us (5%)
  between operations  14.2 us (3%)
  local copies, waits for them, and re-layouts  8.46 us (2%)
  other arithmetic  7.1 us (2%)
    reduce_scatter x1, waiting for transfers between devices, own_rows(): lax.psum_scatter(portion(jnp.int32(0), count), axis, scatter_dimension=0,...  120 us
    reduce_scatter x1, waiting for transfers between devices, body(): lax.psum_scatter(partial_term, 'tp', scatter_dimension=1, tiled=True)  76.2 us
    all_gather x1, waiting for transfers between devices, body(): whole = lax.all_gather(tokens, 'tp', axis=1, tiled=True)  48.5 us
    all_gather x1, waiting for transfers between devices, body(): grads = lax.all_gather(out_grad, 'tp', axis=1, tiled=True)  48.4 us
    all_gather x1, waiting for transfers between devices, body(): lax.all_gather(gate_weight, 'fsdp', axis=0, tiled=True)  37.2 us
    all_gather x1, waiting for transfers between devices, over_all(): lax.all_gather(a, axis, axis=dim, tiled=True)  32.8 us
    all_gather x1, waiting for transfers between devices, body(): lax.all_gather(up_weight, 'fsdp', axis=0, tiled=True)  31.8 us
  transfers between devices with their start and end apart: 7, of which 7 were waited for; matrix products, arithmetic and copies ran while one was open for 4% of the time, Pallas kernels for 0%

commit v1 on v0

--- a/solution.py
+++ b/solution.py
@@ -25,7 +25,15 @@
 
 def body(tokens, out_grad, gate_weight, up_weight, down_weight):
     factor = 1.0 / math.sqrt(tokens.shape[0] * lax.axis_size("fsdp"))
-    whole = lax.all_gather(tokens, "tp", axis=1, tiled=True)
+    lanes = [tokens]
+    ndev = lax.axis_size("tp")
+    for h in range(ndev - 1):
+        e_next = lax.ppermute(
+            lanes[-1], "tp", [(hop_no, (hop_no + 1) % ndev) for hop_no in range(ndev)]
+        )
+        lanes.append(e_next)
+    a_next = jnp.concatenate(lanes[::-1], axis=1)
+    whole = jnp.roll(a_next, (lax.axis_index("tp") + 1) * tokens.shape[1], axis=1)
     grads = lax.all_gather(out_grad, "tp", axis=1, tiled=True)
     gate_full, up_full = (
         lax.all_gather(gate_weight, "fsdp", axis=0, tiled=True),

time: 451 us -> 404 us (0.90)
  waiting for transfers between devices: 398 us -> 331 us
  local copies, waits for them, and re-layouts: 8.46 us -> 23.6 us
    ppermute x0 -> x7, waiting for transfers between devices: none -> 73.9 us  [body(): lax.ppermute(lanes[-1], 'tp', [(hop_no, (hop_no + 1) % ndev) for hop_no i...]
    all_gather x1 -> x0, waiting for transfers between devices: 48.5 us -> none  [body(): whole = lax.all_gather(tokens, 'tp', axis=1, tiled=True)]
    all_gather x1, waiting for transfers between devices: 37.2 us -> 0.01 us  [body(): lax.all_gather(gate_weight, 'fsdp', axis=0, tiled=True)]
    all_gather x1, waiting for transfers between devices: 31.8 us -> 0.02 us  [body(): lax.all_gather(up_weight, 'fsdp', axis=0, tiled=True)]
    all_gather x1, waiting for transfers between devices: 32.8 us -> 10.8 us  [over_all(): lax.all_gather(a, axis, axis=dim, tiled=True)]
    unnamed x10 -> x25, local copies, waits for them, and re-layouts: 5.38 us -> 19.6 us
  transfers between devices with their start and end apart: 7 -> 13, of which waited for: 7 -> 11; matrix products, arithmetic and copies ran while one was open for 4% -> 10% of each run, Pallas kernels for 0% -> 0%
where the time goes in v1:
time: 404 us; the launch traced here: 403 us
  waiting for transfers between devices  331 us (82%)
  matrix products  26.3 us (7%)
  local copies, waits for them, and re-layouts  23.6 us (6%)
  between operations  14.2 us (4%)
  other arithmetic  7.03 us (2%)
    reduce_scatter x1, waiting for transfers between devices, own_rows(): lax.psum_scatter(portion(jnp.int32(0), count), axis, scatter_dimension=0,...  120 us
    reduce_scatter x1, waiting for transfers between devices, body(): lax.psum_scatter(partial_term, 'tp', scatter_dimension=1, tiled=True)  75.8 us
    ppermute x7, waiting for transfers between devices, body(): lax.ppermute(lanes[-1], 'tp', [(hop_no, (hop_no + 1) % ndev) for hop_no i...  73.9 us
    all_gather x1, waiting for transfers between devices, body(): grads = lax.all_gather(out_grad, 'tp', axis=1, tiled=True)  48.4 us
    unnamed x25, local copies, waits for them, and re-layouts  19.6 us
    all_gather x1, waiting for transfers between devices, over_all(): lax.all_gather(a, axis, axis=dim, tiled=True)  10.8 us
  transfers between devices with their start and end apart: 13, of which 11 were waited for; matrix products, arithmetic and copies ran while one was open for 10% of the time, Pallas kernels for 0%

profile of v1, /device:TPU:0, one launch (start us, length us, event | category | flops | bytes accessed | tf_op | source)
XLA Modules:
  0.0 403.3 jit_solution(2693401050739954374)
XLA Ops:
  10.6 11.1 %collective-permute-done = bf16[256,1024]{1,0:T(8,128)(2,1)S(1)} collective-permute-done((bf16[256,1024]{1,0:T(8,128)(2,1)}, bf16[256,1024]{1,0:T(8,128)(2,1)S(1)}, u32[]{:S(2)}, u32[]{:S(2)}) %collective-permute-start) | collective-permute-done | bytes 524320 | tf_op jit(solution)/shard_map/ppermute | solution.py:31
  21.7 10.4 %collective-permute-done.1 = bf16[256,1024]{1,0:T(8,128)(2,1)S(1)} collective-permute-done((bf16[256,1024]{1,0:T(8,128)(2,1)S(1)}, bf16[256,1024]{1,0:T(8,128)(2,1)S(1)}, u32[]{:S(2)}, u32[]{:S(2)}) %collective-permute-start.1) | collective-permute-done | bytes 524320 | tf_op jit(solution)/shard_map/ppermute | solution.py:31
  32.1 10.4 %collective-permute-done.2 = bf16[256,1024]{1,0:T(8,128)(2,1)S(1)} collective-permute-done((bf16[256,1024]{1,0:T(8,128)(2,1)S(1)}, bf16[256,1024]{1,0:T(8,128)(2,1)S(1)}, u32[]{:S(2)}, u32[]{:S(2)}) %collective-permute-start.2) | collective-permute-done | bytes 524320 | tf_op jit(solution)/shard_map/ppermute | solution.py:31
  42.5 10.4 %collective-permute-done.3 = bf16[256,1024]{1,0:T(8,128)(2,1)S(1)} collective-permute-done((bf16[256,1024]{1,0:T(8,128)(2,1)S(1)}, bf16[256,1024]{1,0:T(8,128)(2,1)S(1)}, u32[]{:S(2)}, u32[]{:S(2)}) %collective-permute-start.3) | collective-permute-done | bytes 524320 | tf_op jit(solution)/shard_map/ppermute | solution.py:31
  52.9 10.4 %collective-permute-done.4 = bf16[256,1024]{1,0:T(8,128)(2,1)S(1)} collective-permute-done((bf16[256,1024]{1,0:T(8,128)(2,1)S(1)}, bf16[256,1024]{1,0:T(8,128)(2,1)S(1)}, u32[]{:S(2)}, u32[]{:S(2)}) %collective-permute-start.4) | collective-permute-done | bytes 524320 | tf_op jit(solution)/shard_map/ppermute | solution.py:31
  63.3 10.5 %collective-permute-done.5 = bf16[256,1024]{1,0:T(8,128)(2,1)} collective-permute-done((bf16[256,1024]{1,0:T(8,128)(2,1)S(1)}, bf16[256,1024]{1,0:T(8,128)(2,1)}, u32[]{:S(2)}, u32[]{:S(2)}) %collective-permute-start.5) | collective-permute-done | bytes 524320 | tf_op jit(solution)/shard_map/ppermute | solution.py:31
  73.8 10.7 %collective-permute-done.6 = bf16[256,1024]{1,0:T(8,128)(2,1)} collective-permute-done((bf16[256,1024]{1,0:T(8,128)(2,1)}, bf16[256,1024]{1,0:T(8,128)(2,1)}, u32[]{:S(2)}, u32[]{:S(2)}) %collective-permute-start.6) | collective-permute-done | bytes 524320 | tf_op jit(solution)/shard_map/ppermute | solution.py:31
  84.5 1.9 constant_dynamic-update-slice_fusion.15
  86.4 1.9 constant_dynamic-update-slice_fusion.14
  90.0 0.9 constant_dynamic-update-slice_fusion.11
  91.7 0.9 constant_dynamic-update-slice_fusion.9
  92.5 0.9 constant_dynamic-update-slice_fusion.8
  93.4 2.0 constant_dynamic-update-slice_fusion.7
  95.4 1.9 constant_dynamic-update-slice_fusion.6
  99.8 0.9 constant_dynamic-update-slice_fusion.2
  100.7 0.9 constant_dynamic-update-slice_fusion.1
  102.4 4.2 %fusion.3 = f32[256,128]{1,0:T(8,128)S(1)} fusion(bf16[8192,128]{1,0:T(8,128)(2,1)} %all-gather.11.cloned.1.call-done, bf16[256,16384]{1,0:T(8,128)(2,1)} %constant_dynamic-update-slice_fusion, s32[]{:T(128)S(6)} %select_n.14), kind=kOutput, calls=%fused_computation.8 | convolution fusion | flops 536870912 | bytes 6422532 | tf_op jit(solution)/shard_map/dot_general | solution.py:42
  106.6 4.5 %fusion.5 = f32[256,128]{1,0:T(8,128)S(1)} fusion(bf16[8192,128]{1,0:T(8,128)(2,1)} %all-gather.9.cloned.1.call-done, bf16[256,16384]{1,0:T(8,128)(2,1)} %constant_dynamic-update-slice_fusion, s32[]{:T(128)S(6)} %select_n.14), kind=kOutput, calls=%fused_computation.10 | convolution fusion | flops 536870912 | bytes 6422532 | tf_op jit(solution)/shard_map/dot_general | solution.py:43
  111.1 10.8 %all-gather.7.cloned.1.call-done = bf16[128,8192]{1,0:T(8,128)(2,1)} async-done(((bf16[128,2048]{1,0:T(8,128)(2,1)}), bf16[128,8192]{1,0:T(8,128)(2,1)}) %all-gather.7.cloned.1.call-update) | async-done | bytes 2097168 | tf_op jit(solution)/shard_map/all_gather | solution.py:9
  121.9 48.4 %all-gather.5.cloned.1.call-done = bf16[256,8192]{1,0:T(8,128)(2,1)} async-done(((bf16[256,1024]{1,0:T(8,128)(2,1)}), bf16[256,8192]{1,0:T(8,128)(2,1)}) %all-gather.5.cloned.1.call-update) | async-done | bytes 4194320 | tf_op jit(solution)/shard_map/all_gather | solution.py:37
  170.2 4.2 %multiply_convert_fusion.1 = (bf16[256,128]{1,0:T(8,128)(2,1)S(1)}, bf16[256,128]{1,0:T(8,128)(2,1)S(1)}) fusion(f32[256,128]{1,0:T(8,128)S(1)} %fusion.3, f32[256,128]{1,0:T(8,128)S(1)} %fusion.5, bf16[256,8192]{1,0:T(8,128)(2,1)} %all-gather.5.cloned.1.call-done, bf16[128,8192]{1,0:T(8,128)(2,1)} %all-gather.7.cloned.1.call-done), kind=kOutput, calls=%fused_computation.14 | convolution fusion | flops 537296896 | bytes 6684672 | tf_op jit(solution)/shard_map/dot_general | solution.py:47
  174.5 1.3 fusion.14
  175.8 4.5 %convolution_add_fusion = f32[256,8192]{1,0:T(8,128)} fusion(f32[256,8192]{1,0:T(8,128)S(1)} %fusion.14, bf16[256,128]{1,0:T(8,128)(2,1)S(1)} %get-tuple-element.11, bf16[8192,128]{1,0:T(8,128)(2,1)S(1)} %copy-done.1), kind=kOutput, calls=%fused_computation.1 | convolution fusion | flops 538968064 | bytes 18939904 | tf_op jit(solution)/shard_map/dot_general | solution.py:60
  180.3 3.2 convolution_multiply_fusion.1
  183.5 3.6 convolution_multiply_fusion.2
  187.9 4.9 %pad_maximum_fusion = f32[8192,384]{0,1:T(8,128)} fusion(f32[8192,128]{0,1:T(8,128)S(1)} %fusion, f32[8192,128]{0,1:T(8,128)S(1)} %convolution_multiply_fusion.1, f32[8192,128]{0,1:T(8,128)S(1)} %convolution_multiply_fusion.2), kind=kLoop, calls=%fused_computation | loop fusion | flops 6291456 | bytes 25165824 | tf_op jit(solution)/shard_map/concatenate | solution.py:67
  192.9 75.8 %reduce-scatter.3.cloned.1.call-done = f32[256,1024]{1,0:T(8,128)} async-done(((f32[256,8192]{1,0:T(8,128)}), f32[256,1024]{1,0:T(8,128)}) %reduce-scatter.3.cloned.1.call-update) | async-done | bytes 1048592 | tf_op jit(solution)/shard_map/reduce_scatter | solution.py:61
  268.7 2.1 convert_element_type.14
  270.8 120.0 %reduce-scatter.5.cloned.1.call-done = f32[2048,384]{0,1:T(8,128)} async-done(((f32[8192,384]{0,1:T(8,128)}), f32[2048,384]{0,1:T(8,128)}) %reduce-scatter.5.cloned.1.call-update) | async-done | bytes 3145744 | tf_op jit(solution)/shard_map/reduce_scatter | solution.py:15
  390.8 3.1 slice_bitcast_fusion
  393.9 1.3 copy.9
  395.2 1.3 copy.10
  (37 shorter events, 10.2 us)
Async XLA Ops:
  7.2 85.4 %copy-start.3 = (bf16[256,1024]{1,0:T(8,128)(2,1)S(1)}, bf16[256,1024]{1,0:T(8,128)(2,1)}, u32[]{:S(2)}) copy-start(bf16[256,1024]{1,0:T(8,128)(2,1)} %param.5) | copy-start | bytes 1572868
  7.2 95.2 %all-gather.11.cloned.1.call-start = ((), (), s32[]{:S(2)}) async-start(), calls=%async_computation.5 | async-start | bytes 2621440 | tf_op jit(solution)/shard_map/all_gather | solution.py:39
  7.9 98.7 %all-gather.9.cloned.1.call-start = ((), (), s32[]{:S(2)}) async-start(), calls=%async_computation.4 | async-start | bytes 2621440 | tf_op jit(solution)/shard_map/all_gather | solution.py:40
  8.7 113.2 %all-gather.7.cloned.1.call-start = ((), (), s32[]{:S(2)}) async-start(), calls=%async_computation.3 | async-start | bytes 2621440 | tf_op jit(solution)/shard_map/all_gather | solution.py:9
  9.4 160.8 %all-gather.5.cloned.1.call-start = ((), (), s32[]{:S(2)}) async-start(), calls=%async_computation.2 | async-start | bytes 4718592 | tf_op jit(solution)/shard_map/all_gather | solution.py:37
  10.0 258.8 %reduce-scatter.3.cloned.1.call-start = ((), (), s32[]{:S(2)}) async-start(), calls=%async_computation.6 | async-start | bytes 9437184 | tf_op jit(solution)/shard_map/reduce_scatter | solution.py:61
  10.0 11.6 %collective-permute-start = (bf16[256,1024]{1,0:T(8,128)(2,1)}, bf16[256,1024]{1,0:T(8,128)(2,1)S(1)}, u32[]{:S(2)}, u32[]{:S(2)}) collective-permute-start(bf16[256,1024]{1,0:T(8,128)(2,1)} %param.5), channel_id=1, source_target_pairs={{0,1},{1,2},{2,3},{3,4},{4,5},{5,6},{6,7},{7,0},{8,9},{9,10},{10,1... | collective-permute-start | bytes 1572872 | tf_op jit(solution)/shard_map/ppermute | solution.py:31
  21.7 10.4 %collective-permute-start.1 = (bf16[256,1024]{1,0:T(8,128)(2,1)S(1)}, bf16[256,1024]{1,0:T(8,128)(2,1)S(1)}, u32[]{:S(2)}, u32[]{:S(2)}) collective-permute-start(bf16[256,1024]{1,0:T(8,128)(2,1)S(1)} %collective-permute-done), channel_id=1, source_target_pairs={{0,1},{1,2},{2,3},{3,4},{4,5},{5,6},{6,7},{7,0},{8,9},{9,10},{10,1... | collective-permute-start | bytes 1572872 | tf_op jit(solution)/shard_map/ppermute | solution.py:31
  32.1 10.4 %collective-permute-start.2 = (bf16[256,1024]{1,0:T(8,128)(2,1)S(1)}, bf16[256,1024]{1,0:T(8,128)(2,1)S(1)}, u32[]{:S(2)}, u32[]{:S(2)}) collective-permute-start(bf16[256,1024]{1,0:T(8,128)(2,1)S(1)} %collective-permute-done.1), channel_id=1, source_target_pairs={{0,1},{1,2},{2,3},{3,4},{4,5},{5,6},{6,7},{7,0},{8,9},{9,10},{10,1... | collective-permute-start | bytes 1572872 | tf_op jit(solution)/shard_map/ppermute | solution.py:31
  42.5 10.4 %collective-permute-start.3 = (bf16[256,1024]{1,0:T(8,128)(2,1)S(1)}, bf16[256,1024]{1,0:T(8,128)(2,1)S(1)}, u32[]{:S(2)}, u32[]{:S(2)}) collective-permute-start(bf16[256,1024]{1,0:T(8,128)(2,1)S(1)} %collective-permute-done.2), channel_id=1, source_target_pairs={{0,1},{1,2},{2,3},{3,4},{4,5},{5,6},{6,7},{7,0},{8,9},{9,10},{10,1... | collective-permute-start | bytes 1572872 | tf_op jit(solution)/shard_map/ppermute | solution.py:31
  52.9 10.4 %collective-permute-start.4 = (bf16[256,1024]{1,0:T(8,128)(2,1)S(1)}, bf16[256,1024]{1,0:T(8,128)(2,1)S(1)}, u32[]{:S(2)}, u32[]{:S(2)}) collective-permute-start(bf16[256,1024]{1,0:T(8,128)(2,1)S(1)} %collective-permute-done.3), channel_id=1, source_target_pairs={{0,1},{1,2},{2,3},{3,4},{4,5},{5,6},{6,7},{7,0},{8,9},{9,10},{10,1... | collective-permute-start | bytes 1572872 | tf_op jit(solution)/shard_map/ppermute | solution.py:31
  63.3 10.5 %collective-permute-start.5 = (bf16[256,1024]{1,0:T(8,128)(2,1)S(1)}, bf16[256,1024]{1,0:T(8,128)(2,1)}, u32[]{:S(2)}, u32[]{:S(2)}) collective-permute-start(bf16[256,1024]{1,0:T(8,128)(2,1)S(1)} %collective-permute-done.4), channel_id=1, source_target_pairs={{0,1},{1,2},{2,3},{3,4},{4,5},{5,6},{6,7},{7,0},{8,9},{9,10},{10,1... | collective-permute-start | bytes 1572872 | tf_op jit(solution)/shard_map/ppermute | solution.py:31
  73.8 10.7 %collective-permute-start.6 = (bf16[256,1024]{1,0:T(8,128)(2,1)}, bf16[256,1024]{1,0:T(8,128)(2,1)}, u32[]{:S(2)}, u32[]{:S(2)}) collective-permute-start(bf16[256,1024]{1,0:T(8,128)(2,1)} %collective-permute-done.5), channel_id=1, source_target_pairs={{0,1},{1,2},{2,3},{3,4},{4,5},{5,6},{6,7},{7,0},{8,9},{9,10},{10,1... | collective-permute-start | bytes 1572872 | tf_op jit(solution)/shard_map/ppermute | solution.py:31
  102.4 72.1 %copy-start = (bf16[8192,128]{1,0:T(8,128)(2,1)S(1)}, bf16[8192,128]{1,0:T(8,128)(2,1)}, u32[]{:S(2)}) copy-start(bf16[8192,128]{1,0:T(8,128)(2,1)} %all-gather.11.cloned.1.call-done) | copy-start | bytes 6291460
  170.2 5.5 %copy-start.1 = (bf16[8192,128]{1,0:T(8,128)(2,1)S(1)}, bf16[8192,128]{1,0:T(8,128)(2,1)}, u32[]{:S(2)}) copy-start(bf16[8192,128]{1,0:T(8,128)(2,1)} %all-gather.9.cloned.1.call-done) | copy-start | bytes 6291460
  180.2 210.5 %reduce-scatter.5.cloned.1.call-start = ((), (), s32[]{:S(2)}) async-start(), calls=%async_computation.7 | async-start | bytes 15728640 | tf_op jit(solution)/shard_map/reduce_scatter | solution.py:15
  180.3 6.8 %copy-start.2 = (bf16[256,8192]{1,0:T(8,128)(2,1)S(1)}, bf16[256,8192]{1,0:T(8,128)(2,1)}, u32[]{:S(2)}) copy-start(bf16[256,8192]{1,0:T(8,128)(2,1)} %all-gather.5.cloned.1.call-done) | copy-start | bytes 12582916
Sparse Core Ops, SparseCore 0:
  9.8 37.8 all-gather.10
  49.6 35.1 all-gather.8
  86.7 35.1 all-gather.6
  123.3 46.8 all-gather.4
  180.4 88.3 reduce-scatter.2
  271.7 119.0 reduce-scatter.4
